TPU v7x, 32 devices: a whole 2x2x4 slice. The times are simulated.
32 devices in a mesh: groups: 2 (over y), seq: 4 (over z), heads: 2 (over x), cfg: 2 (over core).
Axes of the slice: x: 2, y: 2, z: 4, core: 2. Of those that a mesh axis runs over, the one named last changes fastest.
Arguments:
- video_tokens: bfloat16 [2, 8, 1152, 1024], P('cfg', ('groups', 'seq'), 'heads'), parts along dimension 1, may hold values from -6 to 6
- text_tokens: bfloat16 [2, 8, 1152, 128], P('cfg', ('groups', 'seq'), 'heads'), parts along dimension 1, may hold values from -6 to 6
- text_length: int32 [2, 8], P('cfg', ('groups', 'seq')), parts along dimension 1, may hold values from 1 to 128
- guide_numer: int32 [8], P(('groups', 'seq')), parts along dimension 0, may hold values from 2 to 8
- guide_denom: int32 [8], P(('groups', 'seq')), parts along dimension 0, may hold values from 4 to 8
- spatial_gain: bfloat16 [1152], replicated, may hold values from 0.25 to 1.75
- spatial_qkv: bfloat16 [3, 1152, 1152], P(None, 'heads'), may hold values from -0.11785113 to 0.11785113
- spatial_out: bfloat16 [1152, 1152], P('heads'), may hold values from -0.1875 to 0.1875
- temporal_gain: bfloat16 [1152], replicated, may hold values from 0.25 to 1.75
- temporal_qkv: bfloat16 [3, 1152, 1152], P(None, 'heads'), may hold values from -0.11785113 to 0.11785113
- temporal_out: bfloat16 [1152, 1152], P('heads'), may hold values from -0.1875 to 0.1875
Outputs:
- guided: bfloat16 [8, 1152, 1024], P(('groups', 'seq'), ('heads', 'cfg')), parts along dimension 0
There are 2 independent parts, one for each index of `groups`. A program takes and returns all parts, laid end to end along the dimension named above; an argument that names none is the same for every part. Nothing has to cross between parts.
Inputs may be any that keep to these rules, and one draw needn't show every extreme that they name: `text_length`: text tokens at or beyond a frame's length are padding.
All inputs are finite; a program needn't handle non-finite values.
Results may differ from a plain program's by a relative error of at most 0.009.
Values may be sent and summed in bfloat16 or wider, within the bound.
A program may use at most 64 MiB of HBM per device.

v0:
```python
import jax
import jax.numpy as jnp
from jax import lax
from jax.sharding import PartitionSpec as P

D = 1152
HEAD_DIM = 72
epsilon = 1e-06


def from_partner(shard, axis, stride):
    return lax.ppermute(shard, axis, [(i, i ^ 1 << stride) for i in range(lax.axis_size(axis))])


def softmax_along(scores, axis):
    top_score = jnp.max(scores, axis=axis, keepdims=True)
    expons = jnp.exp(scores - top_score)
    return (expons / jnp.sum(expons, axis=axis, keepdims=True)).astype(jnp.bfloat16)


def project_piece(piece, gain_vector, weights, parts):
    gain_piece = gain_vector.astype(jnp.float32)
    weight_piece = weights[parts]
    piece_wide = piece.astype(jnp.float32)
    scaled = (piece_wide * gain_piece[None, :, None]).astype(jnp.bfloat16)
    product = jnp.einsum("kod,fdp->fkop", weight_piece, scaled, preferred_element_type=jnp.float32)
    return (product, jnp.sum(piece_wide * piece_wide, axis=1))


def add_mixed(piece, matrix):
    return jnp.einsum("oc,fcp->fop", matrix, piece, preferred_element_type=jnp.float32)


def shards(
    video_tokens,
    text_tokens,
    text_length,
    guide_numer,
    guide_denom,
    spatial_gain,
    spatial_qkv,
    spatial_out,
    temporal_gain,
    temporal_qkv,
    temporal_out,
):
    frame_count = video_tokens.shape[1]
    width = video_tokens.shape[2]
    positions = video_tokens.shape[3]
    text_count = text_tokens.shape[3]
    local_heads = width // HEAD_DIM
    frame_tokens = video_tokens[0]
    frame_text = text_tokens[0]
    video_piece = lax.all_gather(frame_tokens, "heads", axis=1, tiled=True)
    text_piece = lax.all_gather(frame_text, "heads", axis=1, tiled=True)
    video_add, video_sq = project_piece(video_piece, spatial_gain, spatial_qkv, slice(0, 3))
    text_add, text_sq = project_piece(text_piece, spatial_gain, spatial_qkv, slice(1, 3))
    mixed = (video_add * lax.rsqrt(video_sq / D + epsilon)[:, None, None, :]).astype(jnp.bfloat16)
    mixed = mixed.reshape(frame_count, 3, local_heads, HEAD_DIM, positions)
    context = (text_add * lax.rsqrt(text_sq / D + epsilon)[:, None, None, :]).astype(jnp.bfloat16)
    context = context.reshape(frame_count, 2, local_heads, HEAD_DIM, text_count)
    key_rows = jnp.concatenate([mixed[:, 1], context[:, 0]], axis=3)
    value_rows = jnp.concatenate([mixed[:, 2], context[:, 1]], axis=3)
    query_all = mixed[:, 0]
    text_valid = jnp.arange(text_count, dtype=jnp.int32)[None, :] < text_length[0][:, None]
    valid_keys = jnp.concatenate(
        [jnp.ones((frame_count, positions), dtype=bool), text_valid], axis=1
    )
    block_rows = min(512, positions)
    block_count = positions // block_rows
    frame_ids = jnp.repeat(jnp.arange(frame_count, dtype=jnp.int32), block_count)
    block_ids = jnp.tile(jnp.arange(block_count, dtype=jnp.int32), frame_count)

    def block_step(inputs):
        frame_id, block_id = inputs
        query_rows = lax.dynamic_slice_in_dim(
            query_all[frame_id], block_id * block_rows, block_rows, 2
        )
        scores = jnp.einsum(
            "hep,hek->hpk", query_rows, key_rows[frame_id], preferred_element_type=jnp.float32
        )
        scores = scores * HEAD_DIM ** (-0.5)
        scores = jnp.where(valid_keys[frame_id][None, None, :], scores, -jnp.inf)
        weights = softmax_along(scores, 2)
        result = jnp.einsum(
            "hpk,hek->hep", weights, value_rows[frame_id], preferred_element_type=jnp.float32
        )
        return result.astype(jnp.bfloat16)

    attended = lax.map(block_step, (frame_ids, block_ids))
    attended = attended.reshape(frame_count, block_count, local_heads, HEAD_DIM, block_rows)
    attended = jnp.transpose(attended, (0, 2, 3, 1, 4)).reshape(frame_count, width, positions)
    update = add_mixed(lax.all_gather(attended, "heads", axis=1, tiled=True), spatial_out)
    after_spatial = (frame_tokens.astype(jnp.float32) + update).astype(jnp.bfloat16)
    own_rows = lax.all_to_all(after_spatial, "seq", split_axis=2, concat_axis=0, tiled=True)
    frames_all = own_rows.shape[0]
    columns = own_rows.shape[2]
    piece_add, piece_sq = project_piece(
        lax.all_gather(own_rows, "heads", axis=1, tiled=True),
        temporal_gain,
        temporal_qkv,
        slice(0, 3),
    )
    mixed_time = (piece_add * lax.rsqrt(piece_sq / D + epsilon)[:, None, None, :]).astype(
        jnp.bfloat16
    )
    mixed_time = mixed_time.reshape(frames_all, 3, local_heads, HEAD_DIM, columns)
    time_scores = jnp.einsum(
        "fhep,ghep->hfgp", mixed_time[:, 0], mixed_time[:, 1], preferred_element_type=jnp.float32
    )
    time_weights = softmax_along(time_scores * HEAD_DIM ** (-0.5), 2)
    attended_time = jnp.einsum(
        "hfgp,ghep->fhep", time_weights, mixed_time[:, 2], preferred_element_type=jnp.float32
    )
    attended_time = attended_time.astype(jnp.bfloat16).reshape(frames_all, width, columns)
    update_time = add_mixed(
        lax.all_gather(attended_time, "heads", axis=1, tiled=True), temporal_out
    )
    block_out = (own_rows.astype(jnp.float32) + update_time).astype(jnp.bfloat16)
    returned = lax.all_to_all(block_out, "seq", split_axis=0, concat_axis=2, tiled=True)
    half_width = width // 2
    partner = from_partner(returned, "cfg", 0)
    branch_index = lax.axis_index("cfg")
    cond_full = jnp.where(branch_index == 0, returned, partner)
    uncond_full = jnp.where(branch_index == 0, partner, returned)
    cond_part = lax.dynamic_slice_in_dim(cond_full, branch_index * half_width, half_width, 1)
    uncond_part = lax.dynamic_slice_in_dim(uncond_full, branch_index * half_width, half_width, 1)
    ratio = guide_numer.astype(jnp.float32) / guide_denom.astype(jnp.float32)
    cond_wide = cond_part.astype(jnp.float32)
    uncond_wide = uncond_part.astype(jnp.float32)
    return (uncond_wide + ratio[:, None, None] * (cond_wide - uncond_wide)).astype(jnp.bfloat16)


def solution(mesh):
    return jax.shard_map(
        shards,
        mesh=mesh,
        in_specs=(
            P("cfg", ("groups", "seq"), "heads", None),
            P("cfg", ("groups", "seq"), "heads", None),
            P("cfg", ("groups", "seq")),
            P(("groups", "seq")),
            P(("groups", "seq")),
            P(),
            P(None, "heads", None),
            P("heads", None),
            P(),
            P(None, "heads", None),
            P("heads", None),
        ),
        out_specs=P(("groups", "seq"), ("heads", "cfg"), None),
        check_vma=False,
    )
```

profile of v0, /device:TPU:0, one launch (start us, length us, event | category | flops | bytes accessed | tf_op | source)
XLA Modules:
  0.0 359.0 jit_solution(843548291912899709)
XLA Ops:
  6.5 0.0 copy-start
  6.5 0.0 all-gather.12.cloned.1.call-start
  6.5 0.7 all-gather.12.cloned.1.call-update
  7.3 0.0 all-gather.8.cloned.1.call-start
  7.3 0.7 convert_element_type.98
  8.7 7.7 %all-gather.1 = bf16[1,1,1152,128]{3,2,1,0:T(8,128)(2,1)S(1)} all-gather(bf16[1,1,576,128]{3,2,1,0:T(8,128)(2,1)} %param.14), channel_id=3, replica_groups=mesh['groups'=2,'seq'=4,'heads'=2,'cfg'=2] {'heads'}, dimensions={2}, use_global_device_ids=true | all-gather | bytes 442368 | tf_op jit(solution)/shard_map/all_gather | solution.py:55
  16.4 0.2 fusion.93
  16.6 3.0 fusion.87
  19.6 28.1 %all-gather.12.cloned.1.call-done = bf16[1,1,1152,1024]{3,2,1,0:T(8,128)(2,1)} async-done(((bf16[1,1,576,1024]{3,2,1,0:T(8,128)(2,1)}), bf16[1,1,1152,1024]{3,2,1,0:T(8,128)(2,1)}) %all-gather.12.cloned.1.call-update) | async-done | bytes 2359312 | tf_op jit(solution)/shard_map/all_gather | solution.py:54
  47.7 2.3 fusion.50
  50.0 0.0 copy-done.3
  50.1 7.3 %fusion.48 = bf16[1,1024,3,576]{1,3,2,0:T(8,128)(2,1)S(1)} fusion(f32[1024]{0:T(1024)S(1)} %add_rsqrt_fusion.1, bf16[3,576,1152]{2,1,0:T(8,128)(2,1)} %param.19, bf16[1,1,1152,1024]{3,2,1,0:T(8,128)(2,1)S(1)} %copy-done.3, f32[1152]{0:T(1024)S(1)} %convert_element_type.98), kind=kOutput, calls=%fused_computation.28 | convolution fusion | flops 4083941376 | bytes 9888256 | tf_op jit(solution)/shard_map/kod,fdp->fkop/dot_general | solution.py:26
  57.3 1.4 slice_bitcast_fusion
  58.7 1.3 pad_maximum_fusion
  60.1 37.0 %while.10 = (s32[]{:T(128)}, bf16[2,8,72,512]{3,2,1,0:T(8,128)(2,1)}, pred[1,1152]{1,0:T(4,128)(4,1)S(1)}, s32[2]{0:T(128)S(1)}, bf16[1,8,72,1024]{3,2,1,0:T(8,1...) while((s32[]{:T(128)}, ...), condition=%wide.region_5.6_spmd, body=%wide.region_2.5_spmd.sunk | while | flops 2081200384 | bytes 5788856 | solution.py:90
  60.5 0.7 dynamic_slice.50
  61.9 7.0 %exponential_reduce_fusion.2 = f32[8,512]{1,0:T(8,128)S(1)} fusion(pred[1152]{0:T(1024)(128)(4,1)S(1)} %reduce.5, bf16[1,8,72,1152]{3,2,1,0:T(8,128)(2,1)S(1)} %get-tuple-element.139, bf16[1,8,72,1024]{3,2,1,0:T(8,128)(2,1)} %get-tuple-element.138, s32[]{:T(128)S(6)} %select_n.52), kind=kOutput, calls=%fused_computation.5.clone.1 | convolution fusion | flops 698352768 | bytes 1934468 | tf_op jit(solution)/shard_map/while/body/eval_jaxpr/sub | solution.py:17
  69.0 9.8 %fusion.120 = bf16[2,8,72,512]{3,2,1,0:T(8,128)(2,1)} fusion(bf16[2,8,72,512]{3,2,1,0:T(8,128)(2,1)} %get-tuple-element.123, s32[]{:T(128)} %get-tuple-element.122, bf16[1,8,72,1152]{3,2,1,0:T(8,128)(2,1)} %get-tuple-element.140, f32[8,512]{1,0:T(8,128)S(1)} %exponential_reduce_fusion.2, pred[1152]{0:T(1024)(128)(4,1)S(1)} %reduce.5, ...), kind=kOutput, calls=%fused_computation.13.clone.1 | convolution fusion | flops 1382847616 | bytes 3851908 | tf_op jit(solution)/shard_map/while/body/eval_jaxpr/hpk,hek->hep/dot_general | solution.py:85
  78.8 0.7 dynamic_slice.50
  80.2 7.0 %exponential_reduce_fusion.2 = f32[8,512]{1,0:T(8,128)S(1)} fusion(pred[1152]{0:T(1024)(128)(4,1)S(1)} %reduce.5, bf16[1,8,72,1152]{3,2,1,0:T(8,128)(2,1)S(1)} %get-tuple-element.139, bf16[1,8,72,1024]{3,2,1,0:T(8,128)(2,1)} %get-tuple-element.138, s32[]{:T(128)S(6)} %select_n.52), kind=kOutput, calls=%fused_computation.5.clone.1 | convolution fusion | flops 698352768 | bytes 1934468 | tf_op jit(solution)/shard_map/while/body/eval_jaxpr/sub | solution.py:17
  87.2 9.8 %fusion.120 = bf16[2,8,72,512]{3,2,1,0:T(8,128)(2,1)} fusion(bf16[2,8,72,512]{3,2,1,0:T(8,128)(2,1)} %get-tuple-element.123, s32[]{:T(128)} %get-tuple-element.122, bf16[1,8,72,1152]{3,2,1,0:T(8,128)(2,1)} %get-tuple-element.140, f32[8,512]{1,0:T(8,128)S(1)} %exponential_reduce_fusion.2, pred[1152]{0:T(1024)(128)(4,1)S(1)} %reduce.5, ...), kind=kOutput, calls=%fused_computation.13.clone.1 | convolution fusion | flops 1382847616 | bytes 3851908 | tf_op jit(solution)/shard_map/while/body/eval_jaxpr/hpk,hek->hep/dot_general | solution.py:85
  97.1 2.5 copy.43
  99.6 1.7 reshape.105
  101.2 0.0 all-gather.8.cloned.1.call-update
  101.3 0.2 all-gather.14.cloned.1.call-start
  101.5 36.0 %all-gather.8.cloned.1.call-done = bf16[1,1152,1024]{2,1,0:T(8,128)(2,1)} async-done(((bf16[1,576,1024]{2,1,0:T(8,128)(2,1)}), bf16[1,1152,1024]{2,1,0:T(8,128)(2,1)}) %all-gather.8.cloned.1.call-update) | async-done | bytes 2359312 | tf_op jit(solution)/shard_map/all_gather | solution.py:93
  137.5 0.0 copy-done
  137.5 3.7 %fusion.64 = bf16[1,576,1024]{2,1,0:T(8,128)(2,1)S(1)} fusion(bf16[576,1152]{1,0:T(8,128)(2,1)S(1)} %copy-done, bf16[1,1152,1024]{2,1,0:T(8,128)(2,1)} %all-gather.8.cloned.1.call-done, bf16[1,1,576,1024]{3,2,1,0:T(8,128)(2,1)} %param.13), kind=kOutput, calls=%fused_computation.47 | convolution fusion | flops 1360723968 | bytes 6045696 | tf_op jit(solution)/shard_map/oc,fcp->fop/dot_general | solution.py:31
  141.1 4.1 %copy.44 = bf16[1,576,1024]{1,0,2:T(2,128)(2,1)} copy(bf16[1,576,1024]{2,1,0:T(8,128)(2,1)S(1)} %fusion.64) | data formatting | bytes 2359296 | tf_op jit(solution)/shard_map/convert_element_type | solution.py:94
  145.3 0.5 broadcast.82
  145.8 9.9 %reduce.3 = bf16[1024,576]{1,0:T(8,128)(2,1)S(1)} reduce(bf16[1024,1,576]{2,1,0:T(2,128)(2,1)} %bitcast.189, bf16[]{:T(256)} %broadcast.82), dimensions={1}, to_apply=%bitcast.164.reduce_sub_computation | reduce | bytes 2359298
  155.7 2.6 reshape.124
  158.3 33.0 %all_to_all.36 = bf16[4,2,73728]{2,1,0:T(2,128)(2,1)S(1)} all-to-all(bf16[4,2,73728]{2,1,0:T(2,128)(2,1)} %reshape.124), channel_id=1, replica_groups=mesh['groups'=2,'seq'=4,'heads'=2,'cfg'=2] {'seq'}, dimensions={0} | all-to-all | bytes 2359296 | tf_op jit(solution)/shard_map/all_to_all | solution.py:95
  191.3 3.3 reshape.125
  194.5 1.9 copy.57
  196.5 0.0 copy-start.5
  196.5 1.5 copy.46
  197.9 0.0 all-gather.14.cloned.1.call-update
  198.0 0.3 all-gather.10.cloned.1.call-start
  198.2 0.0 copy-done.5
  198.3 34.1 %all-gather.14.cloned.1.call-done = bf16[4,1,1152,256]{3,2,0,1:T(8,128)(2,1)} async-done(((bf16[4,1,576,256]{3,2,0,1:T(8,128)(2,1)}), bf16[4,1,1152,256]{3,2,0,1:T(8,128)(2,1)}) %all-gather.14.cloned.1.call-update) | async-done | bytes 2359312 | tf_op jit(solution)/shard_map/all_gather | solution.py:99
  232.3 2.3 fusion.52
  234.6 0.1 copy-done.4
  234.7 7.2 %multiply_convert_fusion = bf16[4,256,3,576]{1,3,2,0:T(8,128)(2,1)S(1)} fusion(f32[4,256]{1,0:T(4,128)S(1)} %add_rsqrt_fusion, bf16[3,576,1152]{2,1,0:T(8,128)(2,1)} %param.22, bf16[4,1,1152,256]{3,2,0,1:T(8,128)(2,1)S(1)} %copy-done.4, f32[1152]{0:T(1024)S(1)} %convert_element_type.109), kind=kOutput, calls=%fused_computation.29 | convolution fusion | flops 4083941376 | bytes 9888256 | tf_op jit(solution)/shard_map/kod,fdp->fkop/dot_general | solution.py:26
  241.9 1.9 fusion.104
  243.8 2.8 copy.59
  246.7 4.1 %copy.60 = bf16[4,1,8,72,256]{3,0,4,2,1:T(4,128)(2,1)} copy(bf16[4,1,8,72,256]{4,3,2,1,0:T(8,128)(2,1)} %get-tuple-element.59) | data formatting | bytes 2359296
  250.7 5.8 %fusion.71 = f32[8,256,4,4]{3,2,1,0:T(4,128)} fusion(bf16[4,1,8,72,256]{3,0,4,2,1:T(4,128)(2,1)} %copy.60, bf16[4,1,8,72,256]{3,0,4,2,1:T(4,128)(2,1)S(1)} %copy.59), kind=kOutput, calls=%fused_computation.54 | convolution fusion | flops 4718592 | bytes 2490368 | tf_op jit(solution)/shard_map/fhep,ghep->hfgp/dot_general | solution.py:108
  256.5 2.8 copy.50
  259.4 0.0 copy-start.1
  259.5 2.1 copy.51
  261.6 0.0 copy-done.1
  261.6 2.5 copy.58
  264.1 5.8 %convert_bitcast_fusion = bf16[4,8,72,256]{2,0,3,1:T(4,128)(2,1)} fusion(bf16[8,4,4,256]{2,1,3,0:T(4,128)(2,1)} %copy.51, bf16[4,1,8,72,256]{3,0,4,2,1:T(4,128)(2,1)} %copy.58), kind=kOutput, calls=%fused_computation.59 | convolution fusion | flops 5308416 | bytes 2424832 | tf_op jit(solution)/shard_map/hfgp,ghep->fhep/dot_general | solution.py:112
  269.9 4.2 %copy.52 = bf16[4,8,72,256]{3,2,1,0:T(8,128)(2,1)} copy(bf16[4,8,72,256]{2,0,3,1:T(4,128)(2,1)} %convert_bitcast_fusion) | data formatting | bytes 2359296 | tf_op jit(solution)/shard_map/convert_element_type | solution.py:115
  274.1 0.0 all-gather.10.cloned.1.call-update
  274.1 36.2 %all-gather.10.cloned.1.call-done = bf16[4,1152,256]{2,1,0:T(8,128)(2,1)} async-done(((bf16[4,576,256]{2,1,0:T(8,128)(2,1)}), bf16[4,1152,256]{2,1,0:T(8,128)(2,1)}) %all-gather.10.cloned.1.call-update) | async-done | bytes 2359312 | tf_op jit(solution)/shard_map/all_gather | solution.py:117
  310.3 0.0 copy-done.2
  310.3 3.8 %fusion.63 = bf16[4,576,256]{2,1,0:T(8,128)(2,1)S(1)} fusion(bf16[4,1152,256]{2,1,0:T(8,128)(2,1)} %all-gather.10.cloned.1.call-done, bf16[576,1152]{1,0:T(8,128)(2,1)} %param.23, bf16[1,576,4,256]{3,1,2,0:T(8,128)(2,1)S(1)} %copy-done.2), kind=kOutput, calls=%fused_computation.45 | convolution fusion | flops 1360723968 | bytes 6045696 | tf_op jit(solution)/shard_map/oc,fcp->fop/dot_general | solution.py:31
  314.1 32.8 %all_to_all.37 = bf16[4,576,256]{2,1,0:T(8,128)(2,1)S(1)} all-to-all(bf16[4,576,256]{2,1,0:T(8,128)(2,1)S(1)} %fusion.63), channel_id=1, replica_groups=mesh['groups'=2,'seq'=4,'heads'=2,'cfg'=2] {'seq'}, dimensions={0} | all-to-all | bytes 2359296 | tf_op jit(solution)/shard_map/all_to_all | solution.py:120
  346.8 0.1 copy.61
  347.0 0.1 collective-permute-start
  348.4 1.6 collective-permute-done
  350.0 2.2 fusion.91
  (17 shorter events, 0.2 us)
Async XLA Ops:
  6.5 130.9 %copy-start = (bf16[576,1152]{1,0:T(8,128)(2,1)S(1)}, bf16[576,1152]{1,0:T(8,128)(2,1)}, u32[]{:S(2)}) copy-start(bf16[576,1152]{1,0:T(8,128)(2,1)} %param.20) | copy-start | bytes 3981316
  6.5 41.1 %all-gather.12.cloned.1.call-start = ((), (), s32[]{:S(2)}) async-start(), calls=%async_computation.4 | async-start | bytes 3538944 | tf_op jit(solution)/shard_map/all_gather | solution.py:54
  7.3 130.2 %all-gather.8.cloned.1.call-start = ((), (), s32[]{:S(2)}) async-start(), calls=%async_computation.2 | async-start | bytes 3538944 | tf_op jit(solution)/shard_map/all_gather | solution.py:93
  47.7 2.4 copy-start.3
  101.3 131.0 %all-gather.14.cloned.1.call-start = ((), (), s32[]{:S(2)}) async-start(), calls=%async_computation.5 | async-start | bytes 3538944 | tf_op jit(solution)/shard_map/all_gather | solution.py:99
  196.5 1.8 copy-start.5
  198.0 112.3 %all-gather.10.cloned.1.call-start = ((), (), s32[]{:S(2)}) async-start(), calls=%async_computation.3 | async-start | bytes 3538944 | tf_op jit(solution)/shard_map/all_gather | solution.py:117
  232.3 2.4 copy-start.4
  259.4 2.2 copy-start.1
  269.9 40.4 %copy-start.2 = (bf16[1,576,4,256]{3,1,2,0:T(8,128)(2,1)S(1)}, bf16[1,576,4,256]{3,1,2,0:T(8,128)(2,1)}, u32[]{:S(2)}) copy-start(bf16[1,576,4,256]{3,1,2,0:T(8,128)(2,1)} %copy.46) | copy-start | bytes 3538948
  347.0 3.0 collective-permute-start
Sparse Core Ops, SparseCore 0:
  8.9 38.7 all-gather.11
  101.4 36.0 all-gather.7
  198.1 34.1 all-gather.13
  274.2 36.0 all-gather.9
where the time goes:
time: 364 us; the launch traced here: 359 us
  waiting for transfers between devices  137 us (38%)
  blocking collectives  73.5 us (20%)
  matrix products  70.3 us (19%)
  local copies, waits for them, and re-layouts  41.4 us (11%)
  other arithmetic  19.1 us (5%)
  between operations  15.5 us (4%)
    all_gather x1, waiting for transfers between devices, shards(): lax.all_gather(attended_time, 'heads', axis=1, tiled=True)  36.2 us
    all_gather x1, waiting for transfers between devices, shards(): lax.all_gather(attended, 'heads', axis=1, tiled=True)  36 us
    all_gather x1, waiting for transfers between devices, shards(): lax.all_gather(own_rows, 'heads', axis=1, tiled=True)  34.1 us
    all_to_all x1, blocking collectives, shards(): lax.all_to_all(after_spatial, 'seq', split_axis=2, concat_axis=0, tiled=T...  33 us
    all_to_all x1, blocking collectives, shards(): lax.all_to_all(block_out, 'seq', split_axis=0, concat_axis=2, tiled=True)  32.8 us
    all_gather x1, waiting for transfers between devices, shards(): video_piece = lax.all_gather(frame_tokens, 'heads', axis=1, tiled=True)  28.1 us
    dot_general x2, matrix products, block_step(): jnp.einsum('hpk,hek->hep', weights, value_rows[frame_id], preferred_eleme...  19.7 us
    unnamed x19, local copies, waits for them, and re-layouts  17.8 us
  transfers between devices with their start and end apart: 5, of which 5 were waited for; matrix products, arithmetic and copies ran while one was open for 1% of the time, Pallas kernels for 0%

commit v1 on v0

--- a/solution.py
+++ b/solution.py
@@ -6,6 +6,22 @@
 D = 1152
 HEAD_DIM = 72
 epsilon = 1e-06
+
+
+def pairwise_exchange(x, axis, split, join):
+    ways, here = (lax.axis_size(axis), lax.axis_index(axis))
+    width = x.shape[split] // ways
+    shape = list(x.shape)
+    shape[split] = width
+    height = shape[join]
+    shape[join] = height * ways
+    full = jnp.zeros(shape, x.dtype)
+    for mask in range(ways):
+        part = lax.dynamic_slice_in_dim(x, (here ^ mask) * width, width, axis=split)
+        if mask:
+            part = lax.ppermute(part, axis, [(d, d ^ mask) for d in range(ways)])
+        full = lax.dynamic_update_slice_in_dim(full, part, (here ^ mask) * height, axis=join)
+    return full
 
 
 def from_partner(shard, axis, stride):
@@ -92,7 +108,7 @@
     attended = jnp.transpose(attended, (0, 2, 3, 1, 4)).reshape(frame_count, width, positions)
     update = add_mixed(lax.all_gather(attended, "heads", axis=1, tiled=True), spatial_out)
     after_spatial = (frame_tokens.astype(jnp.float32) + update).astype(jnp.bfloat16)
-    own_rows = lax.all_to_all(after_spatial, "seq", split_axis=2, concat_axis=0, tiled=True)
+    own_rows = pairwise_exchange(after_spatial, "seq", 2, 0)
     frames_all = own_rows.shape[0]
     columns = own_rows.shape[2]
     piece_add, piece_sq = project_piece(

time: 364 us -> 334 us (0.918); the launches traced: 359 us -> 333 us
  blocking collectives: 73.5 us -> 40.5 us
  waiting for transfers between devices: 137 us -> 160 us
  other arithmetic: 19.1 us -> 9.16 us
  local copies, waits for them, and re-layouts: 41.4 us -> 31.7 us
  starting transfers between devices: 0.58 us -> 4.87 us
    all_to_all x1 -> x0, blocking collectives: 33 us -> none  [shards(): lax.all_to_all(after_spatial, 'seq', split_axis=2, concat_axis=0, tiled=T...]
    ppermute x0 -> x3, waiting for transfers between devices: none -> 19.6 us  [pairwise_exchange(): part = lax.ppermute(part, axis, [(d, d ^ mask) for d in range(ways)])]
    unnamed x1 -> x0, other arithmetic: 9.93 us -> none
    unnamed x19 -> x17, local copies, waits for them, and re-layouts: 17.8 us -> 10.5 us
    ppermute x0 -> x3, starting transfers between devices: none -> 4.45 us  [pairwise_exchange(): part = lax.ppermute(part, axis, [(d, d ^ mask) for d in range(ways)])]
    convert_element_type x1 -> x0, local copies, waits for them, and re-layouts: 4.11 us -> none  [shards(): (frame_tokens.astype(jnp.float32) + update).astype(jnp.bfloat16)]
    all_gather x1, waiting for transfers between devices: 34.1 us -> 38.1 us  [shards(): lax.all_gather(own_rows, 'heads', axis=1, tiled=True)]
  transfers between devices with their start and end apart: 5 -> 8, of which waited for: 5 -> 7; matrix products, arithmetic and copies ran while one was open for 1% -> 2% of each run, Pallas kernels for 0% -> 0%
where the time goes in v1:
time: 334 us; the launch traced here: 333 us
  waiting for transfers between devices  160 us (48%)
  matrix products  70.3 us (21%)
  blocking collectives  40.5 us (12%)
  local copies, waits for them, and re-layouts  31.7 us (9%)
  between operations  15.4 us (5%)
  other arithmetic  9.16 us (3%)
  starting transfers between devices  4.87 us (1%)
    all_gather x1, waiting for transfers between devices, shards(): lax.all_gather(own_rows, 'heads', axis=1, tiled=True)  38.1 us
    all_gather x1, waiting for transfers between devices, shards(): lax.all_gather(attended_time, 'heads', axis=1, tiled=True)  36.2 us
    all_gather x1, waiting for transfers between devices, shards(): lax.all_gather(attended, 'heads', axis=1, tiled=True)  35.9 us
    all_to_all x1, blocking collectives, shards(): lax.all_to_all(block_out, 'seq', split_axis=0, concat_axis=2, tiled=True)  32.8 us
    all_gather x1, waiting for transfers between devices, shards(): video_piece = lax.all_gather(frame_tokens, 'heads', axis=1, tiled=True)  28.1 us
    dot_general x2, matrix products, block_step(): jnp.einsum('hpk,hek->hep', weights, value_rows[frame_id], preferred_eleme...  19.7 us
    ppermute x3, waiting for transfers between devices, pairwise_exchange(): part = lax.ppermute(part, axis, [(d, d ^ mask) for d in range(ways)])  19.6 us
    dot_general x3, matrix products, project_piece(): jnp.einsum('kod,fdp->fkop', weight_piece, scaled, preferred_element_type=...  17.5 us
  transfers between devices with their start and end apart: 8, of which 7 were waited for; matrix products, arithmetic and copies ran while one was open for 2% of the time, Pallas kernels for 0%

profile of v1, /device:TPU:0, one launch (start us, length us, event | category | flops | bytes accessed | tf_op | source)
XLA Modules:
  0.0 333.5 jit_solution(6464101008968819925)
XLA Ops:
  6.5 0.0 copy-start
  6.5 0.0 all-gather.13.cloned.1.call-start
  6.5 0.7 all-gather.13.cloned.1.call-update
  7.3 0.0 all-gather.7.cloned.1.call-start
  7.3 0.7 convert_element_type.98
  8.7 7.7 %all-gather.1 = bf16[1,1,1152,128]{3,2,1,0:T(8,128)(2,1)S(1)} all-gather(bf16[1,1,576,128]{3,2,1,0:T(8,128)(2,1)} %param.14), channel_id=3, replica_groups=mesh['groups'=2,'seq'=4,'heads'=2,'cfg'=2] {'heads'}, dimensions={2}, use_global_device_ids=true | all-gather | bytes 442368 | tf_op jit(solution)/shard_map/all_gather | solution.py:71
  16.4 0.2 fusion.92
  16.6 3.0 fusion.86
  19.6 28.1 %all-gather.13.cloned.1.call-done = bf16[1,1,1152,1024]{3,2,1,0:T(8,128)(2,1)} async-done(((bf16[1,1,576,1024]{3,2,1,0:T(8,128)(2,1)}), bf16[1,1,1152,1024]{3,2,1,0:T(8,128)(2,1)}) %all-gather.13.cloned.1.call-update) | async-done | bytes 2359312 | tf_op jit(solution)/shard_map/all_gather | solution.py:70
  47.7 2.3 fusion.52
  50.0 0.0 copy-done.4
  50.1 7.3 %fusion.48 = bf16[1,1024,3,576]{1,3,2,0:T(8,128)(2,1)S(1)} fusion(f32[1024]{0:T(1024)S(1)} %add_rsqrt_fusion.1, bf16[3,576,1152]{2,1,0:T(8,128)(2,1)} %param.19, bf16[1,1,1152,1024]{3,2,1,0:T(8,128)(2,1)S(1)} %copy-done.4, f32[1152]{0:T(1024)S(1)} %convert_element_type.98), kind=kOutput, calls=%fused_computation.28 | convolution fusion | flops 4083941376 | bytes 9888256 | tf_op jit(solution)/shard_map/kod,fdp->fkop/dot_general | solution.py:42
  57.3 1.4 slice_bitcast_fusion
  58.7 1.3 pad_maximum_fusion
  60.0 36.4 %while.10 = (s32[]{:T(128)}, bf16[2,8,72,512]{3,2,1,0:T(8,128)(2,1)}, pred[1,1152]{1,0:T(4,128)(4,1)S(1)}, s32[2]{0:T(128)S(1)}, bf16[1,8,72,1024]{3,2,1,0:T(8,1...) while((s32[]{:T(128)}, ...), condition=%wide.region_5.6_spmd, body=%wide.region_2.5_spmd.sunk | while | flops 2081200384 | bytes 5788856 | solution.py:106
  60.0 0.6 dynamic_slice.70
  61.4 7.0 %exponential_reduce_fusion.2 = f32[8,512]{1,0:T(8,128)S(1)} fusion(pred[1152]{0:T(1024)(128)(4,1)S(1)} %reduce.4, bf16[1,8,72,1152]{3,2,1,0:T(8,128)(2,1)S(1)} %get-tuple-element.143, bf16[1,8,72,1024]{3,2,1,0:T(8,128)(2,1)} %get-tuple-element.142, s32[]{:T(128)S(6)} %select_n.84), kind=kOutput, calls=%fused_computation.5.clone.1 | convolution fusion | flops 698352768 | bytes 1934468 | tf_op jit(solution)/shard_map/while/body/eval_jaxpr/sub | solution.py:33
  68.4 9.9 %fusion.119 = bf16[2,8,72,512]{3,2,1,0:T(8,128)(2,1)} fusion(bf16[2,8,72,512]{3,2,1,0:T(8,128)(2,1)} %get-tuple-element.127, s32[]{:T(128)} %get-tuple-element.126, bf16[1,8,72,1152]{3,2,1,0:T(8,128)(2,1)} %get-tuple-element.144, f32[8,512]{1,0:T(8,128)S(1)} %exponential_reduce_fusion.2, pred[1152]{0:T(1024)(128)(4,1)S(1)} %reduce.4, ...), kind=kOutput, calls=%fused_computation.13.clone.1 | convolution fusion | flops 1382847616 | bytes 3851908 | tf_op jit(solution)/shard_map/while/body/eval_jaxpr/hpk,hek->hep/dot_general | solution.py:101
  78.2 0.6 dynamic_slice.70
  79.6 7.0 %exponential_reduce_fusion.2 = f32[8,512]{1,0:T(8,128)S(1)} fusion(pred[1152]{0:T(1024)(128)(4,1)S(1)} %reduce.4, bf16[1,8,72,1152]{3,2,1,0:T(8,128)(2,1)S(1)} %get-tuple-element.143, bf16[1,8,72,1024]{3,2,1,0:T(8,128)(2,1)} %get-tuple-element.142, s32[]{:T(128)S(6)} %select_n.84), kind=kOutput, calls=%fused_computation.5.clone.1 | convolution fusion | flops 698352768 | bytes 1934468 | tf_op jit(solution)/shard_map/while/body/eval_jaxpr/sub | solution.py:33
  86.6 9.8 %fusion.119 = bf16[2,8,72,512]{3,2,1,0:T(8,128)(2,1)} fusion(bf16[2,8,72,512]{3,2,1,0:T(8,128)(2,1)} %get-tuple-element.127, s32[]{:T(128)} %get-tuple-element.126, bf16[1,8,72,1152]{3,2,1,0:T(8,128)(2,1)} %get-tuple-element.144, f32[8,512]{1,0:T(8,128)S(1)} %exponential_reduce_fusion.2, pred[1152]{0:T(1024)(128)(4,1)S(1)} %reduce.4, ...), kind=kOutput, calls=%fused_computation.13.clone.1 | convolution fusion | flops 1382847616 | bytes 3851908 | tf_op jit(solution)/shard_map/while/body/eval_jaxpr/hpk,hek->hep/dot_general | solution.py:101
  96.4 2.5 copy.23
  98.9 1.7 reshape.105
  100.6 0.0 all-gather.7.cloned.1.call-update
  100.6 0.3 all-gather.9.cloned.1.call-start
  100.9 35.9 %all-gather.7.cloned.1.call-done = bf16[1,1152,1024]{2,1,0:T(8,128)(2,1)} async-done(((bf16[1,576,1024]{2,1,0:T(8,128)(2,1)}), bf16[1,1152,1024]{2,1,0:T(8,128)(2,1)}) %all-gather.7.cloned.1.call-update) | async-done | bytes 2359312 | tf_op jit(solution)/shard_map/all_gather | solution.py:109
  136.8 3.7 %fusion.63 = bf16[1,576,1024]{2,1,0:T(8,128)(2,1)S(1)} fusion(bf16[576,1152]{1,0:T(8,128)(2,1)S(1)} %copy-done, bf16[1,1152,1024]{2,1,0:T(8,128)(2,1)} %all-gather.7.cloned.1.call-done, bf16[1,1,576,1024]{3,2,1,0:T(8,128)(2,1)} %param.13), kind=kOutput, calls=%fused_computation.45 | convolution fusion | flops 1360723968 | bytes 6045696 | tf_op jit(solution)/shard_map/oc,fcp->fop/dot_general | solution.py:47
  140.5 0.1 broadcast_in_dim.24
  140.6 0.0 copy-start.6
  140.6 0.2 constant_dynamic-slice_fusion
  140.8 1.6 collective-permute-start
  142.3 2.4 collective-permute-start.1
  144.7 0.5 collective-permute-start.2
  145.2 9.8 %collective-permute-done = bf16[1,576,256]{2,1,0:T(8,128)(2,1)} collective-permute-done((bf16[1,576,256]{2,1,0:T(8,128)(2,1)S(1)}, bf16[1,576,256]{2,1,0:T(8,128)(2,1)}, u32[]{:S(2)}, u32[]{:S(2)}) %collective-permute-start) | collective-permute-done | bytes 294944 | tf_op jit(solution)/shard_map/ppermute | solution.py:22
  155.0 1.0 constant_dynamic-update-slice_fusion.2
  155.9 9.9 %collective-permute-done.1 = bf16[1,576,256]{2,1,0:T(8,128)(2,1)} collective-permute-done((bf16[1,576,256]{2,1,0:T(8,128)(2,1)S(1)}, bf16[1,576,256]{2,1,0:T(8,128)(2,1)}, u32[]{:S(2)}, u32[]{:S(2)}) %collective-permute-start.1) | collective-permute-done | bytes 294944 | tf_op jit(solution)/shard_map/ppermute | solution.py:22
  165.8 1.0 constant_dynamic-update-slice_fusion.1
  166.8 0.0 collective-permute-done.2
  166.8 1.0 constant_dynamic-update-slice_fusion
  167.8 1.0 copy-done.2
  168.9 0.0 all-gather.9.cloned.1.call-update
  168.9 0.0 all-gather.11.cloned.1.call-start
  168.9 0.0 copy-done.6
  169.0 38.1 %all-gather.9.cloned.1.call-done = bf16[4,1152,256]{2,1,0:T(8,128)(2,1)} async-done(((bf16[4,576,256]{2,1,0:T(8,128)(2,1)}), bf16[4,1152,256]{2,1,0:T(8,128)(2,1)}) %all-gather.9.cloned.1.call-update) | async-done | bytes 2359312 | tf_op jit(solution)/shard_map/all_gather | solution.py:115
  207.0 2.3 fusion.50
  209.3 0.1 copy-done.5
  209.4 7.2 %multiply_convert_fusion = bf16[4,256,3,576]{1,3,2,0:T(8,128)(2,1)S(1)} fusion(f32[4,256]{1,0:T(4,128)S(1)} %add_rsqrt_fusion, bf16[3,576,1152]{2,1,0:T(8,128)(2,1)} %param.22, bf16[4,1152,256]{2,1,0:T(8,128)(2,1)S(1)} %copy-done.5, f32[1152]{0:T(1024)S(1)} %convert_element_type.109), kind=kOutput, calls=%fused_computation.29 | convolution fusion | flops 4083941376 | bytes 9888256 | tf_op jit(solution)/shard_map/kod,fdp->fkop/dot_general | solution.py:42
  216.7 1.9 fusion.103
  218.5 2.8 copy.33
  221.4 4.0 %copy.34 = bf16[4,1,8,72,256]{3,0,4,2,1:T(4,128)(2,1)} copy(bf16[4,1,8,72,256]{4,3,2,1,0:T(8,128)(2,1)} %get-tuple-element.59) | data formatting | bytes 2359296
  225.4 5.8 %fusion.70 = f32[8,256,4,4]{3,2,1,0:T(4,128)} fusion(bf16[4,1,8,72,256]{3,0,4,2,1:T(4,128)(2,1)} %copy.34, bf16[4,1,8,72,256]{3,0,4,2,1:T(4,128)(2,1)S(1)} %copy.33), kind=kOutput, calls=%fused_computation.53 | convolution fusion | flops 4718592 | bytes 2490368 | tf_op jit(solution)/shard_map/fhep,ghep->hfgp/dot_general | solution.py:124
  231.3 2.8 copy.27
  234.2 2.0 copy.28
  236.3 2.5 copy.32
  238.7 5.8 %convert_bitcast_fusion = bf16[4,8,72,256]{2,0,3,1:T(4,128)(2,1)} fusion(bf16[8,4,4,256]{2,1,3,0:T(4,128)(2,1)} %copy.28, bf16[4,1,8,72,256]{3,0,4,2,1:T(4,128)(2,1)} %copy.32), kind=kOutput, calls=%fused_computation.58 | convolution fusion | flops 5308416 | bytes 2424832 | tf_op jit(solution)/shard_map/hfgp,ghep->fhep/dot_general | solution.py:128
  244.6 4.2 %copy.29 = bf16[4,8,72,256]{3,2,1,0:T(8,128)(2,1)} copy(bf16[4,8,72,256]{2,0,3,1:T(4,128)(2,1)} %convert_bitcast_fusion) | data formatting | bytes 2359296 | tf_op jit(solution)/shard_map/convert_element_type | solution.py:131
  248.8 0.0 all-gather.11.cloned.1.call-update
  248.8 36.2 %all-gather.11.cloned.1.call-done = bf16[4,1152,256]{2,1,0:T(8,128)(2,1)} async-done(((bf16[4,576,256]{2,1,0:T(8,128)(2,1)}), bf16[4,1152,256]{2,1,0:T(8,128)(2,1)}) %all-gather.11.cloned.1.call-update) | async-done | bytes 2359312 | tf_op jit(solution)/shard_map/all_gather | solution.py:133
  285.0 3.8 %fusion.64 = bf16[4,576,256]{2,1,0:T(8,128)(2,1)S(1)} fusion(bf16[4,576,256]{2,1,0:T(8,128)(2,1)S(1)} %copy-done.3, bf16[4,1152,256]{2,1,0:T(8,128)(2,1)} %all-gather.11.cloned.1.call-done, bf16[576,1152]{1,0:T(8,128)(2,1)} %param.23), kind=kOutput, calls=%fused_computation.47 | convolution fusion | flops 1360723968 | bytes 6045696 | tf_op jit(solution)/shard_map/oc,fcp->fop/dot_general | solution.py:47
  288.8 32.8 %all_to_all.18 = bf16[4,576,256]{2,1,0:T(8,128)(2,1)S(1)} all-to-all(bf16[4,576,256]{2,1,0:T(8,128)(2,1)S(1)} %fusion.64), channel_id=1, replica_groups=mesh['groups'=2,'seq'=4,'heads'=2,'cfg'=2] {'seq'}, dimensions={0} | all-to-all | bytes 2359296 | tf_op jit(solution)/shard_map/all_to_all | solution.py:136
  321.6 0.1 copy.35
  321.7 0.1 collective-permute-start.3
  323.1 1.6 collective-permute-done.3
  324.8 2.2 fusion.90
  (22 shorter events, 0.2 us)
Async XLA Ops:
  6.5 130.3 %copy-start = (bf16[576,1152]{1,0:T(8,128)(2,1)S(1)}, bf16[576,1152]{1,0:T(8,128)(2,1)}, u32[]{:S(2)}) copy-start(bf16[576,1152]{1,0:T(8,128)(2,1)} %param.20) | copy-start | bytes 3981316
  6.5 41.1 %all-gather.13.cloned.1.call-start = ((), (), s32[]{:S(2)}) async-start(), calls=%async_computation.4 | async-start | bytes 3538944 | tf_op jit(solution)/shard_map/all_gather | solution.py:70
  7.3 129.5 %all-gather.7.cloned.1.call-start = ((), (), s32[]{:S(2)}) async-start(), calls=%async_computation.1 | async-start | bytes 3538944 | tf_op jit(solution)/shard_map/all_gather | solution.py:109
  47.7 2.4 copy-start.4
  100.6 106.4 %all-gather.9.cloned.1.call-start = ((), (), s32[]{:S(2)}) async-start(), calls=%async_computation.2 | async-start | bytes 3538944 | tf_op jit(solution)/shard_map/all_gather | solution.py:115
  140.6 28.4 %copy-start.6 = (bf16[1152]{0:T(1024)(128)(2,1)S(1)}, bf16[1152]{0:T(1024)(128)(2,1)}, u32[]{:S(2)}) copy-start(bf16[1152]{0:T(1024)(128)(2,1)} %param.21) | copy-start | bytes 6916
  140.8 14.2 %collective-permute-start = (bf16[1,576,256]{2,1,0:T(8,128)(2,1)S(1)}, bf16[1,576,256]{2,1,0:T(8,128)(2,1)}, u32[]{:S(2)}, u32[]{:S(2)}) collective-permute-start(bf16[1,576,256]{2,1,0:T(8,128)(2,1)S(1)} %get-tuple-element.65), channel_id=1, source_target_pairs={{0,4},{4,0},{8,12},{12,8},{1,5},{5,1},{9,13},{13,9},{2,6},{6,2},{1... | collective-permute-start | bytes 884744 | tf_op jit(solution)/shard_map/ppermute | solution.py:22
  142.3 23.5 %collective-permute-start.1 = (bf16[1,576,256]{2,1,0:T(8,128)(2,1)S(1)}, bf16[1,576,256]{2,1,0:T(8,128)(2,1)}, u32[]{:S(2)}, u32[]{:S(2)}) collective-permute-start(bf16[1,576,256]{2,1,0:T(8,128)(2,1)S(1)} %get-tuple-element.64), channel_id=1, source_target_pairs={{0,8},{4,12},{8,0},{12,4},{1,9},{5,13},{9,1},{13,5},{2,10},{6,14},... | collective-permute-start | bytes 884744 | tf_op jit(solution)/shard_map/ppermute | solution.py:22
  144.7 22.1 %collective-permute-start.2 = (bf16[1,576,256]{2,1,0:T(8,128)(2,1)S(1)}, bf16[1,576,256]{2,1,0:T(8,128)(2,1)}, u32[]{:S(2)}, u32[]{:S(2)}) collective-permute-start(bf16[1,576,256]{2,1,0:T(8,128)(2,1)S(1)} %get-tuple-element.63), channel_id=1, source_target_pairs={{0,12},{4,8},{8,4},{12,0},{1,13},{5,9},{9,5},{13,1},{2,14},{6,10},... | collective-permute-start | bytes 884744 | tf_op jit(solution)/shard_map/ppermute | solution.py:22
  167.8 1.0 copy-start.2
  168.9 116.1 %all-gather.11.cloned.1.call-start = ((), (), s32[]{:S(2)}) async-start(), calls=%async_computation.3 | async-start | bytes 3538944 | tf_op jit(solution)/shard_map/all_gather | solution.py:133
  207.0 2.4 copy-start.5
  234.1 2.1 copy-start.1
  244.6 40.4 %copy-start.3 = (bf16[4,576,256]{2,1,0:T(8,128)(2,1)S(1)}, bf16[4,576,256]{2,1,0:T(8,128)(2,1)}, u32[]{:S(2)}) copy-start(bf16[4,576,256]{2,1,0:T(8,128)(2,1)} %copy-done.2) | copy-start | bytes 3538948
  321.7 3.0 collective-permute-start.3
Sparse Core Ops, SparseCore 0:
  8.9 38.7 all-gather.12
  100.7 36.0 all-gather.6
  169.0 37.9 all-gather.8
  248.9 36.0 all-gather.10
